TPU v7x, 32 devices: a whole 2x2x4 slice. The times are simulated.
32 devices in a mesh: dp: 8 (over z, x), mp: 4 (over y, core).
Axes of the slice: x: 2, y: 2, z: 4, core: 2. Of those that a mesh axis runs over, the one named last changes fastest.
Arguments:
- stats: float32 [4, 64, 256, 256], P('mp', 'dp'), may hold values from -1 to 1, as said below
- prev_roots: float32 [4, 64, 256, 256], P('mp', 'dp'), may hold values from -1 to 2, as said below
- counts: int32 [4, 8], replicated, may hold values from 1 to 8, as said below
- grads: bfloat16 [4, 64, 256, 1024], P(None, 'dp', None, 'mp'), may hold values from -6 to 6
Outputs:
- precond: bfloat16 [4, 64, 256, 1024], P(None, 'dp', None, 'mp')
Inputs may be any that keep to these rules, and one draw needn't show every extreme that they name: Each model shard's live blocks are the first count slots of each of its devices; every count is 1 to 8, 8 is reached on some device, and the counts of one model shard sum to at most 32, which some model shard reaches. `stats`: every block is symmetric positive definite. `prev_roots`: every block is symmetric.
All inputs are finite; a program needn't handle non-finite values.
Results may differ from a plain program's by a relative error of at most 0.0052.
Values may be sent and summed in bfloat16 or wider, within the bound.
A program may use at most 128 MiB of HBM per device.

v0:
```python
import functools

import jax
import jax.numpy as jnp
from jax import lax
from jax.experimental import pallas as pl
from jax.experimental.pallas import tpu as pltpu
from jax.sharding import PartitionSpec as P

NEWTON = 2
MESH = pl.DeviceIdType.MESH


def split(value):
    high = value.astype(jnp.bfloat16)
    return high, (value - high.astype(jnp.float32)).astype(jnp.bfloat16)


def dot(left, right):
    return jnp.dot(left, right, preferred_element_type=jnp.float32)


def product(left, right):
    return dot(left[0], right[0]) + (dot(left[0], right[1]) + dot(left[1], right[0]))


def newton_root(statistic, initial):
    size = initial.shape[-1]
    rows = lax.broadcasted_iota(jnp.int32, (size, size), 0)
    columns = lax.broadcasted_iota(jnp.int32, (size, size), 1)
    identity = jnp.where(rows == columns, 1.25, 0.0).astype(jnp.float32)
    start = split(initial)
    square = split(product(start, start))
    fourth = split(product(square, square))
    moment = product(fourth, split(statistic))
    estimate = start
    for iteration in range(NEWTON):
        step = split(identity - 0.25 * moment)
        result = product(estimate, step)
        if iteration + 1 < NEWTON:
            estimate = split(result)
            double = split(product(step, step))
            moment = product(split(product(double, double)), split(moment))
    return result


def kernel(members, counts, stats, starts, grads, out, a_buf, x_buf, g_buf, roots,
           a_sem, x_sem, g_sem, y_send, y_recv, p_send, p_recv, f_send, f_recv):
    me = lax.axis_index("mp")
    data = lax.axis_index("dp")
    slots = stats.shape[1]
    chips = members // 2
    core = lax.rem(me, 2)
    chip = me // 2
    partner = me + 1 - 2 * core

    def peer(offset, which):
        return lax.rem(chip + offset, chips) * 2 + which

    def a_copy(slot):
        return pltpu.make_async_copy(stats.at[0, slot], a_buf.at[slot], a_sem.at[slot])

    def x_copy(slot):
        return pltpu.make_async_copy(starts.at[0, slot], x_buf.at[slot], x_sem.at[slot])

    def g_copy(owner):
        return pltpu.make_async_copy(grads.at[owner], g_buf.at[owner], g_sem.at[owner])

    def send(owner, slot, target, send_sem, recv_sem):
        return pltpu.make_async_remote_copy(
            src_ref=roots.at[owner, slot], dst_ref=roots.at[owner, slot],
            send_sem=send_sem, recv_sem=recv_sem,
            device_id={"mp": target}, device_id_type=MESH)

    def y_copy(owner, offset, slot):
        return send(owner, slot, peer(offset, core), y_send.at[offset - 1, slot], y_recv.at[offset - 1, slot])

    def p_copy(owner, slot):
        return send(owner, slot, partner, p_send.at[slot], p_recv.at[slot])

    def f_copy(owner, offset, slot):
        return send(owner, slot, partner, f_send.at[offset - 1, slot], f_recv.at[offset - 1, slot])

    for slot in range(slots):
        x_copy(slot).start()
        a_copy(slot).start()
    for owner in range(members):
        g_copy(owner).start()

    barrier = pltpu.get_barrier_semaphore()
    pl.semaphore_signal(barrier, inc=1, device_id={"mp": partner}, device_id_type=MESH)
    for offset in range(1, chips):
        pl.semaphore_signal(barrier, inc=1, device_id={"mp": peer(offset, core)}, device_id_type=MESH)
    pl.semaphore_wait(barrier, chips)

    live_count = counts[me, data]

    @pl.loop(0, slots)
    def _(slot):
        x_copy(slot).wait()
        a_copy(slot).wait()
        root = newton_root(a_buf[slot], x_buf[slot])
        live = jnp.full(root.shape, slot, jnp.int32) < live_count
        roots[me, slot] = jnp.where(live, root, 0.0).astype(jnp.bfloat16)
        for offset in range(1, chips):
            y_copy(me, offset, slot).start()
        p_copy(me, slot).start()

    for owner in range(members):
        g_copy(owner).wait()

    def apply(owner, slot):
        out[owner, slot] = dot(roots[owner, slot], g_buf[owner, slot]).astype(out.dtype)

    @pl.loop(0, slots)
    def _(slot):
        apply(me, slot)
        p_copy(partner, slot).wait_recv()
        apply(partner, slot)

    @pl.loop(0, slots)
    def _(slot):
        for offset in range(1, chips):
            owner = peer(chips - offset, core)
            y_copy(owner, offset, slot).wait_recv()
            f_copy(owner, offset, slot).start()
            apply(owner, slot)
        for offset in range(1, chips):
            owner = peer(chips - offset, 1 - core)
            f_copy(owner, offset, slot).wait_recv()
            apply(owner, slot)

    @pl.loop(0, slots)
    def _(slot):
        p_copy(me, slot).wait_send()
        for offset in range(1, chips):
            y_copy(me, offset, slot).wait_send()
            f_copy(peer(chips - offset, core), offset, slot).wait_send()


def local(members, stats, prev_roots, counts, grads):
    slots, size = stats.shape[1], stats.shape[2]
    chips = members // 2
    block = (slots, size, size)
    return pl.pallas_call(
        functools.partial(kernel, members),
        out_shape=jax.ShapeDtypeStruct(grads.shape, grads.dtype),
        in_specs=[pl.BlockSpec(memory_space=pltpu.SMEM)] + [pl.BlockSpec(memory_space=pl.ANY)] * 3,
        out_specs=pl.BlockSpec(memory_space=pltpu.VMEM),
        scratch_shapes=[
            pltpu.VMEM(block, jnp.float32),
            pltpu.VMEM(block, jnp.float32),
            pltpu.VMEM(grads.shape, grads.dtype),
            pltpu.VMEM((members,) + block, jnp.bfloat16),
            pltpu.SemaphoreType.DMA((slots,)),
            pltpu.SemaphoreType.DMA((slots,)),
            pltpu.SemaphoreType.DMA((members,)),
            pltpu.SemaphoreType.DMA((chips - 1, slots)),
            pltpu.SemaphoreType.DMA((chips - 1, slots)),
            pltpu.SemaphoreType.DMA((slots,)),
            pltpu.SemaphoreType.DMA((slots,)),
            pltpu.SemaphoreType.DMA((chips - 1, slots)),
            pltpu.SemaphoreType.DMA((chips - 1, slots)),
        ],
        compiler_params=pltpu.CompilerParams(
            collective_id=0, has_side_effects=True, vmem_limit_bytes=56 * 1024 * 1024),
    )(counts, stats, prev_roots, grads)


def solution(mesh):
    return jax.shard_map(
        functools.partial(local, mesh.shape["mp"]),
        mesh=mesh,
        in_specs=(
            P("mp", "dp", None, None),
            P("mp", "dp", None, None),
            P(),
            P(None, "dp", None, "mp"),
        ),
        out_specs=P(None, "dp", None, "mp"),
        check_vma=False,
    )
```

profile of v0, /device:TPU:1, one launch (start us, length us, event | category | flops | bytes accessed | tf_op | source)
XLA Modules:
  0.0 41.7 jit_solution(10765239850197921999)
XLA Ops:
  0.0 37.1 %shard_map.46 = bf16[4,8,256,256]{3,2,1,0:T(8,128)(2,1)} custom-call(s32[4,8]{1,0:T(4,128)} %counts.1, f32[1,8,256,256]{3,2,1,0:T(8,128)} %stats.1, f32[1,8,256,256]{3,2,1,0:T(8,128)} %starts.1, bf16[4,8,256,256]{3,2,1,0:T(8,128)(2,1)} %grads.1), custom_call_target="tpu_custom_call" | custom-call | tf_op jit(solution)/shard_map/pallas_call | solution.py:145
  37.1 4.6 %copy.6 = bf16[4,8,256,256]{3,2,1,0:T(8,128)(2,1)} copy(bf16[4,8,256,256]{3,2,1,0:T(8,128)(2,1)} %shard_map.46) | data formatting | bytes 8388608
where the time goes:
time: 42.5 us; the launch traced here: 41.7 us
  Pallas kernels  37.1 us (87%)
  local copies, waits for them, and re-layouts  4.64 us (11%)
    pallas_call x1, Pallas kernels, local(): pl.pallas_call(functools.partial(kernel, members), out_shape=jax.ShapeDty...  37.1 us
    unnamed x1, local copies, waits for them, and re-layouts  4.64 us

commit v1 on v0

--- a/solution.py
+++ b/solution.py
@@ -8,43 +8,34 @@
 from jax.sharding import PartitionSpec as P
 
 NEWTON = 2
+VMEM_BYTES = 67043328 - 65536
 MESH = pl.DeviceIdType.MESH
 
 
-def split(value):
-    high = value.astype(jnp.bfloat16)
-    return high, (value - high.astype(jnp.float32)).astype(jnp.bfloat16)
+def dot(left, right):
+    return jnp.dot(left.astype(jnp.bfloat16), right.astype(jnp.bfloat16), preferred_element_type=jnp.float32)
 
 
-def dot(left, right):
-    return jnp.dot(left, right, preferred_element_type=jnp.float32)
-
-
-def product(left, right):
-    return dot(left[0], right[0]) + (dot(left[0], right[1]) + dot(left[1], right[0]))
+def shifted_square(part):
+    return 2.0 * part + dot(part, part)
 
 
 def newton_root(statistic, initial):
     size = initial.shape[-1]
     rows = lax.broadcasted_iota(jnp.int32, (size, size), 0)
     columns = lax.broadcasted_iota(jnp.int32, (size, size), 1)
-    identity = jnp.where(rows == columns, 1.25, 0.0).astype(jnp.float32)
-    start = split(initial)
-    square = split(product(start, start))
-    fourth = split(product(square, square))
-    moment = product(fourth, split(statistic))
-    estimate = start
+    identity = jnp.where(rows == columns, 1.0, 0.0).astype(jnp.float32)
+    moment = statistic + dot(shifted_square(shifted_square(initial - identity)), statistic)
+    estimate = initial
     for iteration in range(NEWTON):
-        step = split(identity - 0.25 * moment)
-        result = product(estimate, step)
+        change = 0.25 * (identity - moment)
+        estimate = estimate + dot(estimate, change)
         if iteration + 1 < NEWTON:
-            estimate = split(result)
-            double = split(product(step, step))
-            moment = product(split(product(double, double)), split(moment))
-    return result
+            moment = moment + dot(shifted_square(shifted_square(change)), moment)
+    return estimate
 
 
-def kernel(members, counts, stats, starts, grads, out, a_buf, x_buf, g_buf, roots,
+def kernel(members, count_table, stats, starts, grads, out, counts, count_sem, a_buf, x_buf, g_buf, roots,
            a_sem, x_sem, g_sem, y_send, y_recv, p_send, p_recv, f_send, f_recv):
     me = lax.axis_index("mp")
     data = lax.axis_index("dp")
@@ -81,6 +72,8 @@
     def f_copy(owner, offset, slot):
         return send(owner, slot, partner, f_send.at[offset - 1, slot], f_recv.at[offset - 1, slot])
 
+    count_copy = pltpu.make_async_copy(count_table, counts, count_sem)
+    count_copy.start()
     for slot in range(slots):
         x_copy(slot).start()
         a_copy(slot).start()
@@ -93,6 +86,7 @@
         pl.semaphore_signal(barrier, inc=1, device_id={"mp": peer(offset, core)}, device_id_type=MESH)
     pl.semaphore_wait(barrier, chips)
 
+    count_copy.wait()
     live_count = counts[me, data]
 
     @pl.loop(0, slots)
@@ -142,12 +136,15 @@
     slots, size = stats.shape[1], stats.shape[2]
     chips = members // 2
     block = (slots, size, size)
+    out_bytes = grads.size * grads.dtype.itemsize
     return pl.pallas_call(
         functools.partial(kernel, members),
-        out_shape=jax.ShapeDtypeStruct(grads.shape, grads.dtype),
-        in_specs=[pl.BlockSpec(memory_space=pltpu.SMEM)] + [pl.BlockSpec(memory_space=pl.ANY)] * 3,
+        out_shape=pltpu.VMEM(grads.shape, grads.dtype),
+        in_specs=[pl.BlockSpec(memory_space=pltpu.HBM)] * 4,
         out_specs=pl.BlockSpec(memory_space=pltpu.VMEM),
         scratch_shapes=[
+            pltpu.SMEM(counts.shape, counts.dtype),
+            pltpu.SemaphoreType.DMA,
             pltpu.VMEM(block, jnp.float32),
             pltpu.VMEM(block, jnp.float32),
             pltpu.VMEM(grads.shape, grads.dtype),
@@ -163,7 +160,7 @@
             pltpu.SemaphoreType.DMA((chips - 1, slots)),
         ],
         compiler_params=pltpu.CompilerParams(
-            collective_id=0, has_side_effects=True, vmem_limit_bytes=56 * 1024 * 1024),
+            collective_id=0, has_side_effects=True, vmem_limit_bytes=VMEM_BYTES - out_bytes),
     )(counts, stats, prev_roots, grads)
 
 

time: 42.5 us -> 32.3 us (0.76); the launches traced: 41.7 us -> 32.2 us
  Pallas kernels: 37.1 us -> 30.1 us
  local copies, waits for them, and re-layouts: 4.64 us -> 2.02 us
    pallas_call x1, Pallas kernels: 37.1 us -> 30.1 us  [local(): pl.pallas_call(functools.partial(kernel, members), out_shape=pltpu.VMEM(g...]
    unnamed x1, local copies, waits for them, and re-layouts: 4.64 us -> 2.02 us
where the time goes in v1:
time: 32.3 us; the launch traced here: 32.2 us
  Pallas kernels  30.1 us (93%)
  local copies, waits for them, and re-layouts  2.02 us (6%)
    pallas_call x1, Pallas kernels, local(): pl.pallas_call(functools.partial(kernel, members), out_shape=pltpu.VMEM(g...  30.1 us
    unnamed x1, local copies, waits for them, and re-layouts  2.02 us

profile of v1, /device:TPU:1, one launch (start us, length us, event | category | flops | bytes accessed | tf_op | source)
XLA Modules:
  0.0 32.2 jit_solution(8458341455760150092)
XLA Ops:
  0.0 30.1 %shard_map.46 = bf16[4,8,256,256]{3,2,1,0:T(8,128)(2,1)S(1)} custom-call(s32[4,8]{1,0:T(4,128)} %count_table.1, f32[1,8,256,256]{3,2,1,0:T(8,128)} %stats.1, f32[1,8,256,256]{3,2,1,0:T(8,128)} %starts.1, bf16[4,8,256,256]{3,2,1,0:T(8,128)(2,1)} %grads.1), custom_call_target="tpu_custom_call" | custom-call | tf_op jit(solution)/shard_map/pallas_call | solution.py:140
  30.2 2.0 %copy.6 = bf16[4,8,256,256]{3,2,1,0:T(8,128)(2,1)} copy(bf16[4,8,256,256]{3,2,1,0:T(8,128)(2,1)S(1)} %shard_map.46) | data formatting | bytes 8388608

commit v2 on v1

--- a/solution.py
+++ b/solution.py
@@ -8,6 +8,7 @@
 from jax.sharding import PartitionSpec as P
 
 NEWTON = 2
+PIECES = 1
 VMEM_BYTES = 67043328 - 65536
 MESH = pl.DeviceIdType.MESH
 
@@ -57,48 +58,68 @@
     def g_copy(owner):
         return pltpu.make_async_copy(grads.at[owner], g_buf.at[owner], g_sem.at[owner])
 
-    def send(owner, slot, target, send_sem, recv_sem):
+    def send(block, target, send_sem, recv_sem):
         return pltpu.make_async_remote_copy(
-            src_ref=roots.at[owner, slot], dst_ref=roots.at[owner, slot],
-            send_sem=send_sem, recv_sem=recv_sem,
+            src_ref=block, dst_ref=block, send_sem=send_sem, recv_sem=recv_sem,
             device_id={"mp": target}, device_id_type=MESH)
 
-    def y_copy(owner, offset, slot):
-        return send(owner, slot, peer(offset, core), y_send.at[offset - 1, slot], y_recv.at[offset - 1, slot])
+    height = roots.shape[2] // PIECES
+
+    def strip(piece):
+        return pl.ds(pl.multiple_of(piece * height, height), height)
+
+    def y_copy(owner, offset, slot, piece):
+        at = offset - 1, slot, piece
+        return send(roots.at[owner, slot, strip(piece)], peer(offset, core), y_send.at[at], y_recv.at[at])
 
     def p_copy(owner, slot):
-        return send(owner, slot, partner, p_send.at[slot], p_recv.at[slot])
-
-    def f_copy(owner, offset, slot):
-        return send(owner, slot, partner, f_send.at[offset - 1, slot], f_recv.at[offset - 1, slot])
+        return send(roots.at[owner, slot], partner, p_send.at[slot], p_recv.at[slot])
+
+    def f_copy(owner, offset, slot, piece):
+        at = offset - 1, slot, piece
+        return send(roots.at[owner, slot, strip(piece)], partner, f_send.at[at], f_recv.at[at])
 
     count_copy = pltpu.make_async_copy(count_table, counts, count_sem)
+    x_copy(0).start()
+    a_copy(0).start()
     count_copy.start()
-    for slot in range(slots):
+
+    barrier = pltpu.get_barrier_semaphore()
+    pl.semaphore_signal(barrier, inc=1, device_id={"mp": partner}, device_id_type=MESH)
+    for offset in range(1, chips):
+        pl.semaphore_signal(barrier, inc=1, device_id={"mp": peer(offset, core)}, device_id_type=MESH)
+
+    count_copy.wait()
+    live_count = counts[me, data]
+
+    def compute(slot):
+        root = newton_root(a_buf[slot], x_buf[slot])
+        live = jnp.full(root.shape, slot, jnp.int32) < live_count
+        roots[me, slot] = jnp.where(live, root, 0.0).astype(jnp.bfloat16)
+
+    def launch(slot):
+        for piece in range(PIECES):
+            for offset in range(1, chips):
+                y_copy(me, offset, slot, piece).start()
+        p_copy(me, slot).start()
+
+    x_copy(0).wait()
+    a_copy(0).wait()
+    for slot in range(1, slots):
         x_copy(slot).start()
         a_copy(slot).start()
     for owner in range(members):
         g_copy(owner).start()
-
-    barrier = pltpu.get_barrier_semaphore()
-    pl.semaphore_signal(barrier, inc=1, device_id={"mp": partner}, device_id_type=MESH)
-    for offset in range(1, chips):
-        pl.semaphore_signal(barrier, inc=1, device_id={"mp": peer(offset, core)}, device_id_type=MESH)
+    compute(0)
     pl.semaphore_wait(barrier, chips)
-
-    count_copy.wait()
-    live_count = counts[me, data]
-
-    @pl.loop(0, slots)
+    launch(0)
+
+    @pl.loop(1, slots)
     def _(slot):
         x_copy(slot).wait()
         a_copy(slot).wait()
-        root = newton_root(a_buf[slot], x_buf[slot])
-        live = jnp.full(root.shape, slot, jnp.int32) < live_count
-        roots[me, slot] = jnp.where(live, root, 0.0).astype(jnp.bfloat16)
-        for offset in range(1, chips):
-            y_copy(me, offset, slot).start()
-        p_copy(me, slot).start()
+        compute(slot)
+        launch(slot)
 
     for owner in range(members):
         g_copy(owner).wait()
@@ -112,24 +133,41 @@
         p_copy(partner, slot).wait_recv()
         apply(partner, slot)
 
-    @pl.loop(0, slots)
-    def _(slot):
+    def apply_strip(owner, slot, piece):
+        part = strip(piece)
+        out[owner, slot, part] = dot(roots[owner, slot, part], g_buf[owner, slot]).astype(out.dtype)
+
+    def arrive(count):
+        slot, piece = count // PIECES, lax.rem(count, PIECES)
         for offset in range(1, chips):
             owner = peer(chips - offset, core)
-            y_copy(owner, offset, slot).wait_recv()
-            f_copy(owner, offset, slot).start()
-            apply(owner, slot)
+            y_copy(owner, offset, slot, piece).wait_recv()
+            f_copy(owner, offset, slot, piece).start()
+            apply_strip(owner, slot, piece)
+
+    def passed(count):
+        slot, piece = count // PIECES, lax.rem(count, PIECES)
         for offset in range(1, chips):
             owner = peer(chips - offset, 1 - core)
-            f_copy(owner, offset, slot).wait_recv()
-            apply(owner, slot)
+            f_copy(owner, offset, slot, piece).wait_recv()
+            apply_strip(owner, slot, piece)
+
+    arrive(jnp.int32(0))
+
+    @pl.loop(1, slots * PIECES)
+    def _(count):
+        arrive(count)
+        passed(count - 1)
+
+    passed(jnp.int32(slots * PIECES - 1))
 
     @pl.loop(0, slots)
     def _(slot):
         p_copy(me, slot).wait_send()
-        for offset in range(1, chips):
-            y_copy(me, offset, slot).wait_send()
-            f_copy(peer(chips - offset, core), offset, slot).wait_send()
+        for piece in range(PIECES):
+            for offset in range(1, chips):
+                y_copy(me, offset, slot, piece).wait_send()
+                f_copy(peer(chips - offset, core), offset, slot, piece).wait_send()
 
 
 def local(members, stats, prev_roots, counts, grads):
@@ -152,12 +190,12 @@
             pltpu.SemaphoreType.DMA((slots,)),
             pltpu.SemaphoreType.DMA((slots,)),
             pltpu.SemaphoreType.DMA((members,)),
-            pltpu.SemaphoreType.DMA((chips - 1, slots)),
-            pltpu.SemaphoreType.DMA((chips - 1, slots)),
-            pltpu.SemaphoreType.DMA((slots,)),
-            pltpu.SemaphoreType.DMA((slots,)),
-            pltpu.SemaphoreType.DMA((chips - 1, slots)),
-            pltpu.SemaphoreType.DMA((chips - 1, slots)),
+            pltpu.SemaphoreType.DMA((chips - 1, slots, PIECES)),
+            pltpu.SemaphoreType.DMA((chips - 1, slots, PIECES)),
+            pltpu.SemaphoreType.DMA((slots,)),
+            pltpu.SemaphoreType.DMA((slots,)),
+            pltpu.SemaphoreType.DMA((chips - 1, slots, PIECES)),
+            pltpu.SemaphoreType.DMA((chips - 1, slots, PIECES)),
         ],
         compiler_params=pltpu.CompilerParams(
             collective_id=0, has_side_effects=True, vmem_limit_bytes=VMEM_BYTES - out_bytes),

time: 32.3 us -> 32.3 us (level)
  no operation moved by 1% of the time
where the time goes in v2:
time: 32.3 us; the launch traced here: 32.2 us
  Pallas kernels  30.1 us (93%)
  local copies, waits for them, and re-layouts  2.02 us (6%)
    pallas_call x1, Pallas kernels, local(): pl.pallas_call(functools.partial(kernel, members), out_shape=pltpu.VMEM(g...  30.1 us
    unnamed x1, local copies, waits for them, and re-layouts  2.02 us

profile of v2, /device:TPU:1, one launch (start us, length us, event | category | flops | bytes accessed | tf_op | source)
XLA Modules:
  0.0 32.2 jit_solution(8942792139735262943)
XLA Ops:
  0.0 30.1 %shard_map.46 = bf16[4,8,256,256]{3,2,1,0:T(8,128)(2,1)S(1)} custom-call(s32[4,8]{1,0:T(4,128)} %count_table.1, f32[1,8,256,256]{3,2,1,0:T(8,128)} %stats.1, f32[1,8,256,256]{3,2,1,0:T(8,128)} %starts.1, bf16[4,8,256,256]{3,2,1,0:T(8,128)(2,1)} %grads.1), custom_call_target="tpu_custom_call" | custom-call | tf_op jit(solution)/shard_map/pallas_call | solution.py:178
  30.1 2.0 %copy.6 = bf16[4,8,256,256]{3,2,1,0:T(8,128)(2,1)} copy(bf16[4,8,256,256]{3,2,1,0:T(8,128)(2,1)S(1)} %shard_map.46) | data formatting | bytes 8388608
